TPU v7x, 32 devices: a whole 2x2x4 slice. The times are simulated.
32 devices in a mesh: seq: 16 (over z, y, core), dp: 2 (over x).
Axes of the slice: x: 2, y: 2, z: 4, core: 2. Of those that a mesh axis runs over, the one named last changes fastest.
Arguments:
- q_student: bfloat16 [2, 8192, 1536], P('dp', 'seq'), may hold values from -8 to 8
- kv_student: bfloat16 [2, 128, 3072], P('dp', 'seq'), may hold values from -8 to 8
- q_target: bfloat16 [2, 8192, 1536], P('dp', 'seq'), may hold values from -8 to 8
- kv_target: bfloat16 [2, 128, 3072], P('dp', 'seq'), may hold values from -8 to 8
Outputs:
- student_out: bfloat16 [2, 8192, 1536], P('dp', 'seq')
- target_out: bfloat16 [2, 8192, 1536], P('dp', 'seq')
- distill_loss: float32 [], replicated
All inputs are finite; a program needn't handle non-finite values.
Results may differ from a plain program's by a relative error of at most 0.004.
Values may be sent and summed in bfloat16 or wider, within the bound.
A program may use at most 128 MiB of HBM per device.

v0:
```python
import jax
import jax.numpy as jnp
from jax import lax
from jax.sharding import PartitionSpec as P

HEADS = 12
HD = 128


def absorb(query3, carried, incoming):
    running_max, running_sum, running_out = carried
    block_pairs = incoming[0]
    key_rows = block_pairs.shape[0]
    feature_width = HEADS * HD
    key_block = block_pairs[:, :feature_width].reshape(key_rows, HEADS, HD)
    value_block = block_pairs[:, feature_width:].reshape(key_rows, HEADS, HD)
    scores = jnp.einsum("qhd,khd->hqk", query3, key_block, preferred_element_type=jnp.float32) * (
        1.0 / HD**0.5
    )
    new_max = jnp.maximum(running_max, jnp.max(scores, axis=-1))
    shrink = jnp.exp(running_max - new_max)
    exponent = jnp.exp(scores - new_max[:, :, None])
    running_sum = jnp.sum(exponent, axis=-1)
    running_out = jnp.einsum(
        "hqk,khd->hqd",
        exponent.astype(jnp.bfloat16),
        value_block,
        preferred_element_type=jnp.float32,
    )
    return (new_max, running_sum, running_out)


def normalize(carried, query_rows):
    running_max, running_sum, running_out = carried
    mixed_rows = running_out / running_sum[:, :, None]
    return jnp.transpose(mixed_rows, (1, 0, 2)).reshape(query_rows, HEADS * HD)


def body(q_student, kv_student, q_target, kv_target):
    query_rows = q_student.shape[1]
    student_query = q_student[0].reshape(query_rows, HEADS, HD)
    target_query = q_target[0].reshape(query_rows, HEADS, HD)
    initial = (
        jnp.full((HEADS, query_rows), -1e30, jnp.float32),
        jnp.zeros((HEADS, query_rows), jnp.float32),
        jnp.zeros((HEADS, query_rows, HD), jnp.float32),
    )
    student_all = lax.all_gather(kv_student, "seq", axis=1, tiled=True)
    target_all = lax.all_gather(kv_target, "seq", axis=1, tiled=True)
    student_carry = absorb(student_query, initial, student_all)
    target_carry = absorb(target_query, initial, target_all)
    student_rows = normalize(student_carry, query_rows)
    target_rows = normalize(target_carry, query_rows)
    seq_count = lax.axis_size("seq")
    all_tokens = query_rows * seq_count
    position = (lax.axis_index("seq") * query_rows + jnp.arange(query_rows)).astype(jnp.float32)
    weight = 1.0 + 2.0 * position / float(max(all_tokens - 1, 1))
    gap_rows = student_rows - target_rows
    local_term = jnp.sum(weight[:, None] * gap_rows * gap_rows) / float(all_tokens * HEADS * HD)
    clip_term = lax.psum(local_term, "seq")
    distill_loss = lax.psum(clip_term, "dp")
    return (
        student_rows[None].astype(jnp.bfloat16),
        target_rows[None].astype(jnp.bfloat16),
        distill_loss,
    )


def solution(mesh):
    return jax.shard_map(
        body,
        mesh=mesh,
        in_specs=(
            P("dp", "seq", None),
            P("dp", "seq", None),
            P("dp", "seq", None),
            P("dp", "seq", None),
        ),
        out_specs=(P("dp", "seq", None), P("dp", "seq", None), P()),
        check_vma=False,
    )
```

profile of v0, /device:TPU:0, one launch (start us, length us, event | category | flops | bytes accessed | tf_op | source)
XLA Modules:
  0.0 106.9 jit_solution(2824079883674600560)
XLA Ops:
  0.6 0.0 copy-start
  0.6 25.9 %all_gather.7 = bf16[1,128,3072]{2,1,0:T(8,128)(2,1)S(1)} all-gather(bf16[1,8,3072]{2,1,0:T(8,128)(2,1)} %param.7), channel_id=1, replica_groups=mesh['seq'=16,'dp'=2] {'seq'}, dimensions={1}, use_global_device_ids=true | all-gather | bytes 835584 | tf_op jit(solution)/shard_map/all_gather | solution.py:49
  26.5 0.4 copy.33
  26.9 0.8 fusion.13
  27.7 0.0 copy-done
  27.7 0.7 copy.32
  28.4 0.0 copy-start.4
  28.4 0.6 multiply_reduce_fusion
  29.1 0.6 fusion.3
  29.6 0.0 copy-done.4
  29.6 0.0 copy-start.6
  29.6 2.5 %bitcast_divide_fusion = f32[512,12,128]{0,2,1:T(8,128)} fusion(bf16[128,12,128]{0,2,1:T(8,128)(2,1)S(1)} %bitcast.31, f32[12,512,128]{1,2,0:T(8,128)S(1)} %get-tuple-element.22, f32[512,12]{0,1:T(8,128)S(1)} %bitcast.33, f32[12,512]{1,0:T(8,128)S(1)} %broadcast_maximum_fusion), kind=kOutput, calls=%fused_computation.2 | convolution fusion | flops 204472320 | bytes 6733824 | tf_op jit(solution)/shard_map/hqk,khd->hqd/dot_general | solution.py:24
  32.2 0.0 copy-done.6
  32.2 0.0 copy-start.1
  32.2 19.7 %all_gather.6 = bf16[1,128,3072]{2,1,0:T(8,128)(2,1)S(1)} all-gather(bf16[1,8,3072]{2,1,0:T(8,128)(2,1)S(1)} %copy-done.6), channel_id=1, replica_groups=mesh['seq'=16,'dp'=2] {'seq'}, dimensions={1}, use_global_device_ids=true | all-gather | bytes 835584 | tf_op jit(solution)/shard_map/all_gather | solution.py:48
  51.9 0.4 copy.28
  52.3 0.8 fusion.14
  53.1 0.0 copy-done.1
  53.1 1.6 %copy.27 = bf16[1,512,1536]{1,2,0:T(8,128)(2,1)} copy(bf16[1,512,1536]{2,1,0:T(8,128)(2,1)S(1)} %copy-done.1) | data formatting | bytes 3145728 | tf_op args[0]
  54.7 2.0 %multiply_reduce_fusion.1 = (f32[12,512]{1,0:T(8,128)S(1)}, f32[12,512,128]{1,2,0:T(8,128)S(1)}) fusion(bf16[512,12,128]{0,2,1:T(8,128)(2,1)} %bitcast.23, bf16[128,12,128]{0,2,1:T(8,128)(2,1)S(1)} %bitcast.29), kind=kOutput, calls=%fused_computation.7 | convolution fusion | flops 202893312 | bytes 5136384 | tf_op jit(solution)/shard_map/qhd,khd->hqk/dot_general | solution.py:17
  56.7 0.0 copy-start.3
  56.7 0.0 copy-start.5
  56.7 0.6 copy-done.5
  57.3 1.2 %fusion.1 = f32[12,512]{1,0:T(8,128)} fusion(f32[12,512,128]{1,2,0:T(8,128)S(1)} %get-tuple-element.20, f32[12,512]{1,0:T(8,128)S(1)} %broadcast_maximum_fusion.1), kind=kLoop, calls=%fused_computation.8 | loop fusion | flops 2353152 | bytes 3194880 | tf_op jit(solution)/shard_map/reduce_sum | solution.py:23
  58.5 0.0 copy-done.3
  58.5 6.3 %fusion = (f32[]{:T(128)}, bf16[512,12,128]{0,2,1:T(8,128)(2,1)}, bf16[512,12,128]{0,2,1:T(8,128)(2,1)}) fusion(f32[512,12,128]{0,2,1:T(8,128)} %bitcast_divide_fusion, f32[512]{0:T(512)S(1)} %multiply_add_fusion, f32[512,12]{0,1:T(8,128)} %bitcast.32, bf16[128,12,128]{0,2,1:T(8,128)(2,1)S(1)} %bitcast.30, f32[12,512,128]{1,2,0:T(8,128)S(1)} %get-tuple-element.20, ...), kind=kOutput, calls=%fused_computation.1 | convolution fusion | flops 209190912 | bytes 9881604 | tf_op jit(solution)/shard_map/hqk,khd->hqd/dot_general | solution.py:24
  64.8 0.0 copy-start.2
  64.8 2.7 %copy.37 = bf16[1,512,1536]{2,1,0:T(8,128)(2,1)} copy(bf16[1,512,1536]{1,2,0:T(8,128)(2,1)} %bitcast.27) | data formatting | bytes 3145728
  67.5 0.0 copy-done.2
  67.5 1.6 %copy.38 = bf16[1,512,1536]{2,1,0:T(8,128)(2,1)} copy(bf16[1,512,1536]{1,2,0:T(8,128)(2,1)S(1)} %bitcast.26) | data formatting | bytes 3145728
  69.7 31.7 %psum.14 = f32[]{:T(128)} all-reduce(f32[]{:T(128)S(6)} %div.39), channel_id=1, replica_groups=mesh['seq'=16,'dp'=2] {'seq'}, use_global_device_ids=true, to_apply=%region_5.0 | all-reduce | flops 1 | bytes 8 | tf_op jit(solution)/shard_map/psum | solution.py:60
  101.4 5.5 %psum.15 = f32[]{:T(128)} all-reduce(f32[]{:T(128)} %psum.14), channel_id=1, replica_groups=mesh['seq'=16,'dp'=2] {'dp'}, use_global_device_ids=true, to_apply=%region_6.0 | all-reduce | flops 1 | bytes 8 | tf_op jit(solution)/shard_map/psum | solution.py:61
  (3 shorter events, 0.0 us)
Async XLA Ops:
  0.6 27.1 %copy-start = (bf16[1,512,1536]{2,1,0:T(8,128)(2,1)S(1)}, bf16[1,512,1536]{2,1,0:T(8,128)(2,1)}, u32[]{:S(2)}) copy-start(bf16[1,512,1536]{2,1,0:T(8,128)(2,1)} %param.6) | copy-start | bytes 4718596
  28.4 1.2 %copy-start.4 = (bf16[128,1536]{0,1:T(8,128)(2,1)S(1)}, bf16[128,1536]{0,1:T(8,128)(2,1)}, u32[]{:S(2)}) copy-start(bf16[128,1536]{0,1:T(8,128)(2,1)} %get-tuple-element.16) | copy-start | bytes 1179652
  29.6 2.5 %copy-start.6 = (bf16[1,8,3072]{2,1,0:T(8,128)(2,1)S(1)}, bf16[1,8,3072]{2,1,0:T(8,128)(2,1)}, u32[]{:S(2)}) copy-start(bf16[1,8,3072]{2,1,0:T(8,128)(2,1)} %param.5) | copy-start | bytes 147460
  32.2 20.9 %copy-start.1 = (bf16[1,512,1536]{2,1,0:T(8,128)(2,1)S(1)}, bf16[1,512,1536]{2,1,0:T(8,128)(2,1)}, u32[]{:S(2)}) copy-start(bf16[1,512,1536]{2,1,0:T(8,128)(2,1)} %param.4) | copy-start | bytes 4718596
  56.7 1.8 %copy-start.3 = (bf16[128,1536]{0,1:T(8,128)(2,1)S(1)}, bf16[128,1536]{0,1:T(8,128)(2,1)}, u32[]{:S(2)}) copy-start(bf16[128,1536]{0,1:T(8,128)(2,1)} %get-tuple-element.18) | copy-start | bytes 1179652
  56.7 0.6 copy-start.5
  64.8 2.7 %copy-start.2 = (bf16[512,12,128]{0,2,1:T(8,128)(2,1)S(1)}, bf16[512,12,128]{0,2,1:T(8,128)(2,1)}, u32[]{:S(2)}) copy-start(bf16[512,12,128]{0,2,1:T(8,128)(2,1)} %get-tuple-element.13) | copy-start | bytes 4718596
where the time goes:
time: 107 us
  blocking collectives  82.8 us (77%)
  matrix products  11.5 us (11%)
  local copies, waits for them, and re-layouts  9.49 us (9%)
  other arithmetic  1.75 us (2%)
  between operations  1.39 us (1%)
    psum x1, blocking collectives, body(): clip_term = lax.psum(local_term, 'seq')  31.7 us
    all_gather x1, blocking collectives, body(): target_all = lax.all_gather(kv_target, 'seq', axis=1, tiled=True)  25.9 us
    all_gather x1, blocking collectives, body(): student_all = lax.all_gather(kv_student, 'seq', axis=1, tiled=True)  19.7 us
    dot_general x2, matrix products, absorb(): jnp.einsum('hqk,khd->hqd', exponent.astype(jnp.bfloat16), value_block, pr...  8.79 us
    unnamed x18, local copies, waits for them, and re-layouts  7.15 us
    psum x1, blocking collectives, body(): distill_loss = lax.psum(clip_term, 'dp')  5.54 us
    dot_general x2, matrix products, absorb(): jnp.einsum('qhd,khd->hqk', query3, key_block, preferred_element_type=jnp....  2.66 us

commit v1 on v0

--- a/solution.py
+++ b/solution.py
@@ -58,7 +58,11 @@
     gap_rows = student_rows - target_rows
     local_term = jnp.sum(weight[:, None] * gap_rows * gap_rows) / float(all_tokens * HEADS * HD)
     clip_term = lax.psum(local_term, "seq")
-    distill_loss = lax.psum(clip_term, "dp")
+
+    def heaps_close(local, mesh_dim):
+        return jnp.sum(jax.lax.all_gather(local, axis_name=mesh_dim), 0)
+
+    distill_loss = heaps_close(clip_term, mesh_dim="dp")
     return (
         student_rows[None].astype(jnp.bfloat16),
         target_rows[None].astype(jnp.bfloat16),

time: 107 us -> 110 us (1.028)
  local copies, waits for them, and re-layouts: 9.49 us -> 11.4 us
    psum x1 -> x0, blocking collectives: 5.54 us -> none  [body(): distill_loss = lax.psum(clip_term, 'dp')]
    unnamed x0 -> x1, blocking collectives: none -> 4.91 us
    unnamed x18 -> x23, local copies, waits for them, and re-layouts: 7.15 us -> 9.02 us
where the time goes in v1:
time: 110 us
  blocking collectives  82.8 us (75%)
  matrix products  11.5 us (10%)
  local copies, waits for them, and re-layouts  11.4 us (10%)
  other arithmetic  2.35 us (2%)
  between operations  1.52 us (1%)
    psum x1, blocking collectives, body(): clip_term = lax.psum(local_term, 'seq')  32.3 us
    all_gather x1, blocking collectives, body(): target_all = lax.all_gather(kv_target, 'seq', axis=1, tiled=True)  25.9 us
    all_gather x1, blocking collectives, body(): student_all = lax.all_gather(kv_student, 'seq', axis=1, tiled=True)  19.7 us
    unnamed x23, local copies, waits for them, and re-layouts  9.02 us
    dot_general x2, matrix products, absorb(): jnp.einsum('hqk,khd->hqd', exponent.astype(jnp.bfloat16), value_block, pr...  8.8 us
    unnamed x1, blocking collectives  4.91 us
    dot_general x2, matrix products, absorb(): jnp.einsum('qhd,khd->hqk', query3, key_block, preferred_element_type=jnp....  2.66 us

profile of v1, /device:TPU:0, one launch (start us, length us, event | category | flops | bytes accessed | tf_op | source)
XLA Modules:
  0.0 109.5 jit_solution(6555222530492951649)
XLA Ops:
  0.6 0.0 copy-start
  0.6 25.9 %all_gather.13 = bf16[1,128,3072]{2,1,0:T(8,128)(2,1)S(1)} all-gather(bf16[1,8,3072]{2,1,0:T(8,128)(2,1)} %param.7), channel_id=1, replica_groups=mesh['seq'=16,'dp'=2] {'seq'}, dimensions={1}, use_global_device_ids=true | all-gather | bytes 835584 | tf_op jit(solution)/shard_map/all_gather | solution.py:49
  26.5 0.4 copy.33
  26.9 0.8 fusion.13
  27.7 0.0 copy-done
  27.7 0.7 copy.32
  28.4 0.0 copy-start.4
  28.4 0.6 multiply_reduce_fusion
  29.1 0.6 fusion.3
  29.6 0.0 copy-done.4
  29.6 0.0 copy-start.6
  29.6 2.5 %bitcast_divide_fusion = f32[512,12,128]{0,2,1:T(8,128)} fusion(bf16[128,12,128]{0,2,1:T(8,128)(2,1)S(1)} %bitcast.33, f32[12,512,128]{1,2,0:T(8,128)S(1)} %get-tuple-element.22, f32[512,12]{0,1:T(8,128)S(1)} %bitcast.35, f32[12,512]{1,0:T(8,128)S(1)} %broadcast_maximum_fusion), kind=kOutput, calls=%fused_computation.2 | convolution fusion | flops 204472320 | bytes 6733824 | tf_op jit(solution)/shard_map/hqk,khd->hqd/dot_general | solution.py:24
  32.2 0.0 copy-done.6
  32.2 0.0 copy-start.1
  32.2 19.7 %all_gather.12 = bf16[1,128,3072]{2,1,0:T(8,128)(2,1)S(1)} all-gather(bf16[1,8,3072]{2,1,0:T(8,128)(2,1)S(1)} %copy-done.6), channel_id=1, replica_groups=mesh['seq'=16,'dp'=2] {'seq'}, dimensions={1}, use_global_device_ids=true | all-gather | bytes 835584 | tf_op jit(solution)/shard_map/all_gather | solution.py:48
  51.9 0.4 copy.28
  52.3 0.8 fusion.14
  53.1 0.0 copy-done.1
  53.1 1.6 %copy.27 = bf16[1,512,1536]{1,2,0:T(8,128)(2,1)} copy(bf16[1,512,1536]{2,1,0:T(8,128)(2,1)S(1)} %copy-done.1) | data formatting | bytes 3145728 | tf_op args[0]
  54.7 2.0 %multiply_reduce_fusion.1 = (f32[12,512]{1,0:T(8,128)S(1)}, f32[12,512,128]{1,2,0:T(8,128)S(1)}) fusion(bf16[512,12,128]{0,2,1:T(8,128)(2,1)} %bitcast.25, bf16[128,12,128]{0,2,1:T(8,128)(2,1)S(1)} %bitcast.31), kind=kOutput, calls=%fused_computation.7 | convolution fusion | flops 202893312 | bytes 5136384 | tf_op jit(solution)/shard_map/qhd,khd->hqk/dot_general | solution.py:17
  56.7 0.0 copy-start.3
  56.7 0.0 copy-start.5
  56.7 0.6 copy-done.5
  57.3 1.2 %fusion.1 = f32[12,512]{1,0:T(8,128)} fusion(f32[12,512,128]{1,2,0:T(8,128)S(1)} %get-tuple-element.20, f32[12,512]{1,0:T(8,128)S(1)} %broadcast_maximum_fusion.1), kind=kLoop, calls=%fused_computation.8 | loop fusion | flops 2353152 | bytes 3194880 | tf_op jit(solution)/shard_map/reduce_sum | solution.py:23
  58.5 0.0 copy-done.3
  58.5 0.0 copy-start.7
  58.5 6.3 %fusion = (f32[]{:T(128)}, bf16[512,12,128]{0,2,1:T(8,128)(2,1)}, bf16[512,12,128]{0,2,1:T(8,128)(2,1)}) fusion(f32[512,12,128]{0,2,1:T(8,128)} %bitcast_divide_fusion, f32[512]{0:T(512)S(1)} %multiply_add_fusion, f32[512,12]{0,1:T(8,128)} %bitcast.34, bf16[128,12,128]{0,2,1:T(8,128)(2,1)S(1)} %bitcast.32, f32[12,512,128]{1,2,0:T(8,128)S(1)} %get-tuple-element.20, ...), kind=kOutput, calls=%fused_computation.1 | convolution fusion | flops 209190912 | bytes 9881604 | tf_op jit(solution)/shard_map/hqk,khd->hqd/dot_general | solution.py:24
  64.8 0.0 copy-start.2
  65.5 32.3 %psum.7 = f32[1]{0:T(128)} all-reduce(f32[1]{0:T(128)} %bitcast.14), channel_id=1, replica_groups=mesh['seq'=16,'dp'=2] {'seq'}, use_global_device_ids=true, to_apply=%region_5.0 | all-reduce | flops 1 | bytes 8 | tf_op jit(solution)/shard_map/psum | solution.py:60
  97.9 0.0 copy-done.7
  97.9 0.6 dynamic-slice
  98.5 1.4 %dynamic-update-slice = f32[2]{0:T(128)S(1)} dynamic-update-slice(f32[2]{0:T(128)S(1)} %broadcast.33, f32[1]{0:T(128)} %psum.7, u32[]{:T(128)} %bitcast.15) | dynamic-update-slice | bytes 12
  99.9 4.9 %all-reduce = f32[2]{0:T(128)S(1)} all-reduce(f32[2]{0:T(128)S(1)} %dynamic-update-slice), channel_id=1, replica_groups=mesh['seq'=16,'dp'=2] {'dp'}, use_global_device_ids=true, to_apply=%add | all-reduce | flops 2 | bytes 16
  104.8 0.6 reduce_sum.39
  105.4 2.6 %copy.37 = bf16[1,512,1536]{2,1,0:T(8,128)(2,1)} copy(bf16[1,512,1536]{1,2,0:T(8,128)(2,1)} %bitcast.29) | data formatting | bytes 3145728
  108.0 0.0 copy-done.2
  108.0 1.6 %copy.38 = bf16[1,512,1536]{2,1,0:T(8,128)(2,1)} copy(bf16[1,512,1536]{1,2,0:T(8,128)(2,1)S(1)} %bitcast.28) | data formatting | bytes 3145728
  (4 shorter events, 0.0 us)
Async XLA Ops:
  0.6 27.1 %copy-start = (bf16[1,512,1536]{2,1,0:T(8,128)(2,1)S(1)}, bf16[1,512,1536]{2,1,0:T(8,128)(2,1)}, u32[]{:S(2)}) copy-start(bf16[1,512,1536]{2,1,0:T(8,128)(2,1)} %param.6) | copy-start | bytes 4718596
  28.4 1.2 %copy-start.4 = (bf16[128,1536]{0,1:T(8,128)(2,1)S(1)}, bf16[128,1536]{0,1:T(8,128)(2,1)}, u32[]{:S(2)}) copy-start(bf16[128,1536]{0,1:T(8,128)(2,1)} %get-tuple-element.16) | copy-start | bytes 1179652
  29.6 2.5 %copy-start.6 = (bf16[1,8,3072]{2,1,0:T(8,128)(2,1)S(1)}, bf16[1,8,3072]{2,1,0:T(8,128)(2,1)}, u32[]{:S(2)}) copy-start(bf16[1,8,3072]{2,1,0:T(8,128)(2,1)} %param.5) | copy-start | bytes 147460
  32.2 20.9 %copy-start.1 = (bf16[1,512,1536]{2,1,0:T(8,128)(2,1)S(1)}, bf16[1,512,1536]{2,1,0:T(8,128)(2,1)}, u32[]{:S(2)}) copy-start(bf16[1,512,1536]{2,1,0:T(8,128)(2,1)} %param.4) | copy-start | bytes 4718596
  56.7 1.8 %copy-start.3 = (bf16[128,1536]{0,1:T(8,128)(2,1)S(1)}, bf16[128,1536]{0,1:T(8,128)(2,1)}, u32[]{:S(2)}) copy-start(bf16[128,1536]{0,1:T(8,128)(2,1)} %get-tuple-element.18) | copy-start | bytes 1179652
  56.7 0.6 copy-start.5
  58.5 39.4 %copy-start.7 = (u32[32]{0:T(128)S(1)}, u32[32]{0:T(128)}, u32[]{:S(2)}) copy-start(u32[32]{0:T(128)} %constant.32) | copy-start | bytes 388
  64.8 43.2 %copy-start.2 = (bf16[512,12,128]{0,2,1:T(8,128)(2,1)S(1)}, bf16[512,12,128]{0,2,1:T(8,128)(2,1)}, u32[]{:S(2)}) copy-start(bf16[512,12,128]{0,2,1:T(8,128)(2,1)} %get-tuple-element.13) | copy-start | bytes 4718596

commit v2 on v0

--- a/solution.py
+++ b/solution.py
@@ -5,6 +5,14 @@
 
 HEADS = 12
 HD = 128
+
+
+def assign_face_by_axis(x_local, vector):
+    return jnp.split(
+        lax.all_gather(jnp.concatenate([vector, x_local], 0), "seq", axis=1, tiled=True),
+        [vector.shape[0]],
+        0,
+    )
 
 
 def absorb(query3, carried, incoming):
@@ -45,8 +53,7 @@
         jnp.zeros((HEADS, query_rows), jnp.float32),
         jnp.zeros((HEADS, query_rows, HD), jnp.float32),
     )
-    student_all = lax.all_gather(kv_student, "seq", axis=1, tiled=True)
-    target_all = lax.all_gather(kv_target, "seq", axis=1, tiled=True)
+    student_all, target_all = assign_face_by_axis(kv_target, kv_student)
     student_carry = absorb(student_query, initial, student_all)
     target_carry = absorb(target_query, initial, target_all)
     student_rows = normalize(student_carry, query_rows)

time: 107 us -> 123 us (1.15)
  blocking collectives: 82.8 us -> 37.4 us
  waiting for transfers between devices: 0 us -> 40.1 us
  between operations: 1.39 us -> 14.8 us
  local copies, waits for them, and re-layouts: 9.49 us -> 20.6 us
  matrix products: 11.5 us -> 6.74 us
    all_gather x2 -> x0, blocking collectives: 45.6 us -> none  [the longest x1 25.9 us: body(): target_all = lax.all_gather(kv_target, 'seq', axis=1, tiled=True)]
    all_gather x0 -> x1, waiting for transfers between devices: none -> 40.1 us  [assign_face_by_axis(): lax.all_gather(jnp.concatenate([vector, x_local], 0), 'seq', axis=1, tile...]
    dot_general x2, matrix products: 8.79 us -> 2.64 us  [absorb(): jnp.einsum('hqk,khd->hqd', exponent.astype(jnp.bfloat16), value_block, pr...]
    unnamed x18 -> x10, local copies, waits for them, and re-layouts: 7.15 us -> 13.3 us
    split x0 -> x1, local copies, waits for them, and re-layouts: none -> 5.34 us  [assign_face_by_axis(): jnp.split(lax.all_gather(jnp.concatenate([vector, x_local], 0), 'seq', ax...]
    dot_general x2, matrix products: 2.66 us -> 4.1 us  [absorb(): jnp.einsum('qhd,khd->hqk', query3, key_block, preferred_element_type=jnp....]
  transfers between devices with their start and end apart: 0 -> 1, of which waited for: 0 -> 1; matrix products, arithmetic and copies ran while one was open for 0% -> 3% of each run, Pallas kernels for 0% -> 0%
where the time goes in v2:
time: 123 us; the launch traced here: 122 us
  waiting for transfers between devices  40.1 us (33%)
  blocking collectives  37.4 us (30%)
  local copies, waits for them, and re-layouts  20.6 us (17%)
  between operations  14.8 us (12%)
  matrix products  6.74 us (5%)
  other arithmetic  2.7 us (2%)
    all_gather x1, waiting for transfers between devices, assign_face_by_axis(): lax.all_gather(jnp.concatenate([vector, x_local], 0), 'seq', axis=1, tile...  40.1 us
    psum x1, blocking collectives, body(): clip_term = lax.psum(local_term, 'seq')  31.8 us
    unnamed x10, local copies, waits for them, and re-layouts  13.3 us
    psum x1, blocking collectives, body(): distill_loss = lax.psum(clip_term, 'dp')  5.54 us
    split x1, local copies, waits for them, and re-layouts, assign_face_by_axis(): jnp.split(lax.all_gather(jnp.concatenate([vector, x_local], 0), 'seq', ax...  5.34 us
    dot_general x2, matrix products, absorb(): jnp.einsum('qhd,khd->hqk', query3, key_block, preferred_element_type=jnp....  4.1 us
    dot_general x2, matrix products, absorb(): jnp.einsum('hqk,khd->hqd', exponent.astype(jnp.bfloat16), value_block, pr...  2.64 us
  transfers between devices with their start and end apart: 1, of which 1 were waited for; matrix products, arithmetic and copies ran while one was open for 3% of the time, Pallas kernels for 0%

profile of v2, /device:TPU:0, one launch (start us, length us, event | category | flops | bytes accessed | tf_op | source)
XLA Modules:
  0.0 122.3 jit_solution(5500302214122509078)
XLA Ops:
  7.2 0.0 copy-start
  7.2 0.0 all-gather.2.cloned.1.call-start
  7.2 0.9 pad_maximum_fusion
  8.2 0.7 copy.27
  8.9 0.0 all-gather.2.cloned.1.call-update
  8.9 2.6 %copy.34 = bf16[1,512,1536]{1,2,0:T(8,128)(2,1)} copy(bf16[1,512,1536]{2,1,0:T(8,128)(2,1)} %param.6) | data formatting | bytes 3145728 | tf_op args[2]
  11.5 0.0 copy-done
  11.5 1.6 %copy.29 = bf16[1,512,1536]{1,2,0:T(8,128)(2,1)} copy(bf16[1,512,1536]{2,1,0:T(8,128)(2,1)S(1)} %copy-done) | data formatting | bytes 3145728 | tf_op args[0]
  13.1 40.1 %all-gather.2.cloned.1.call-done = bf16[2,128,3072]{2,0,1:T(2,128)(2,1)} async-done(((bf16[2,8,3072]{2,0,1:T(2,128)(2,1)}), bf16[2,128,3072]{2,0,1:T(2,128)(2,1)}) %all-gather.2.cloned.1.call-update) | async-done | bytes 1572880 | tf_op jit(solution)/shard_map/all_gather | solution.py:12
  53.2 5.3 %fusion.15 = (bf16[1,128,3072]{2,0,1:T(2,128)(2,1)S(1)}, bf16[1,128,3072]{2,0,1:T(2,128)(2,1)}) fusion(bf16[2,128,3072]{2,0,1:T(2,128)(2,1)} %all-gather.2.cloned.1.call-done), kind=kLoop, calls=%fused_computation.24 | loop fusion | bytes 3145728 | tf_op jit(solution)/shard_map/split | solution.py:11
  58.5 1.8 %copy.47 = bf16[1,128,3072]{1,2,0:T(8,128)(2,1)S(1)} copy(bf16[1,128,3072]{2,0,1:T(2,128)(2,1)S(1)} %get-tuple-element.15) | data formatting | bytes 1572864
  60.3 0.1 fusion.16
  60.4 2.1 %bitcast_reduce_fusion = (f32[12,512]{1,0:T(8,128)S(1)}, f32[12,128,512]{2,1,0:T(8,128)S(1)}) fusion(bf16[128,12,128]{0,2,1:T(8,128)(2,1)S(1)} %bitcast.50, bf16[512,12,128]{0,2,1:T(8,128)(2,1)} %bitcast.45), kind=kOutput, calls=%fused_computation.4 | convolution fusion | flops 202893312 | bytes 5136384 | tf_op jit(solution)/shard_map/qhd,khd->hqk/dot_general | solution.py:25
  62.4 0.6 broadcast_maximum_fusion
  63.0 4.2 %copy.46 = bf16[1,128,3072]{1,2,0:T(8,128)(2,1)} copy(bf16[1,128,3072]{2,0,1:T(2,128)(2,1)} %get-tuple-element.16) | data formatting | bytes 1572864
  67.2 0.0 copy-start.1
  67.2 1.2 fusion.17
  68.4 2.0 %bitcast_reduce_fusion.1 = (f32[12,512]{1,0:T(8,128)S(1)}, f32[12,128,512]{2,1,0:T(8,128)S(1)}) fusion(bf16[128,12,128]{0,2,1:T(8,128)(2,1)S(1)} %bitcast.51, bf16[512,12,128]{0,2,1:T(8,128)(2,1)} %bitcast.44), kind=kOutput, calls=%fused_computation.8 | convolution fusion | flops 202893312 | bytes 5136384 | tf_op jit(solution)/shard_map/qhd,khd->hqk/dot_general | solution.py:25
  70.5 0.0 copy-done.1
  70.5 0.6 fusion.5
  71.0 0.9 bitcast_divide_fusion
  71.9 0.6 fusion.3
  72.5 1.8 %fusion = (f32[]{:T(128)}, bf16[512,12,128]{0,2,1:T(8,128)(2,1)S(1)}, bf16[512,12,128]{0,2,1:T(8,128)(2,1)S(1)}) fusion(f32[512,12,128]{0,2,1:T(8,128)S(1)} %bitcast_divide_fusion, f32[512]{0:T(512)S(1)} %multiply_add_fusion, f32[512,12]{0,1:T(8,128)S(1)} %bitcast.54, bf16[128,12,128]{0,2,1:T(8,128)(2,1)S(1)} %bitcast.53, ...), kind=kOutput, calls=%fused_computation.1 | convolution fusion | flops 209190912 | bytes 9881604 | tf_op jit(solution)/shard_map/hqk,khd->hqd/dot_general | solution.py:32
  74.9 1.6 %copy.38 = bf16[1,512,1536]{2,1,0:T(8,128)(2,1)} copy(bf16[1,512,1536]{1,2,0:T(8,128)(2,1)S(1)} %bitcast.49) | data formatting | bytes 3145728
  76.5 31.8 %psum.14 = f32[]{:T(128)} all-reduce(f32[]{:T(128)S(6)} %div.39), channel_id=1, replica_groups=mesh['seq'=16,'dp'=2] {'seq'}, use_global_device_ids=true, to_apply=%region_5.0 | all-reduce | flops 1 | bytes 8 | tf_op jit(solution)/shard_map/psum | solution.py:67
  108.3 1.6 %copy.39 = bf16[1,512,1536]{2,1,0:T(8,128)(2,1)} copy(bf16[1,512,1536]{1,2,0:T(8,128)(2,1)S(1)} %bitcast.48) | data formatting | bytes 3145728
  109.9 5.5 %psum.15 = f32[]{:T(128)} all-reduce(f32[]{:T(128)} %psum.14), channel_id=1, replica_groups=mesh['seq'=16,'dp'=2] {'dp'}, use_global_device_ids=true, to_apply=%region_6.0 | all-reduce | flops 1 | bytes 8 | tf_op jit(solution)/shard_map/psum | solution.py:68
  (2 shorter events, 0.0 us)
Async XLA Ops:
  7.2 4.4 %copy-start = (bf16[1,512,1536]{2,1,0:T(8,128)(2,1)S(1)}, bf16[1,512,1536]{2,1,0:T(8,128)(2,1)}, u32[]{:S(2)}) copy-start(bf16[1,512,1536]{2,1,0:T(8,128)(2,1)} %param.4) | copy-start | bytes 4718596
  7.2 46.0 %all-gather.2.cloned.1.call-start = ((), (), s32[]{:S(2)}) async-start(), calls=%async_computation | async-start | bytes 1671168 | tf_op jit(solution)/shard_map/all_gather | solution.py:12
  67.2 3.2 %copy-start.1 = (f32[12,512]{1,0:T(8,128)S(1)}, f32[12,512]{1,0:T(8,128)}, u32[]{:S(2)}) copy-start(f32[12,512]{1,0:T(8,128)} %broadcast_maximum_fusion) | copy-start | bytes 73732
Sparse Core Ops, SparseCore 0:
  10.8 42.3 all-gather.1
